TPU v7x, 512 devices: a whole 4x8x8 slice. The times are simulated.
512 devices in a mesh: attn: 16 (over y, core), expert: 32 (over z, x).
Axes of the slice: x: 4, y: 8, z: 8, core: 2. Of those that a mesh axis runs over, the one named last changes fastest.
Arguments:
- queries: bfloat16 [4096, 4096], P('attn', 'expert'), may hold values from -90 to 90
- keys: bfloat16 [2, 4096, 128], P(None, 'attn'), may hold values from -10 to 10
- values: bfloat16 [2, 4096, 128], P(None, 'attn'), may hold values from -6 to 6
- residual: bfloat16 [4096, 2048], P(('attn', 'expert')), may hold values from -6 to 6
- prompt_lengths: int32 [4], replicated, may hold values from 1 to 3072, 4096 in all
- out_proj: bfloat16 [4096, 2048], P('expert'), may hold values from -0.5 to 0.5
- norm_gain: float32 [2048], replicated, may hold values from 0.1 to 1.9
- expert_ids: int32 [4096, 8], P(('attn', 'expert')), may hold values from 0 to 127, all different within a row; in each aligned block of 8 rows (0 to 7, 8 to 15, ...) at most 2 rows name the same one
- route_weights: float32 [4096, 8], P(('attn', 'expert')), may hold values from 0.02 to 0.4
- w_gate: bfloat16 [32, 2048, 6144], P('expert', None, 'attn'), may hold values from -0.125 to 0.125
- w_up: bfloat16 [32, 2048, 6144], P('expert', None, 'attn'), may hold values from -0.125 to 0.125
- w_down: bfloat16 [32, 6144, 2048], P('expert', 'attn'), may hold values from -0.15625 to 0.15625
Outputs:
- out: bfloat16 [4096, 2048], P(('attn', 'expert'))
Inputs may be any that keep to these rules, and one draw needn't show every extreme that they name: `prompt_lengths`: the prompts lie end to end and fill all 4096 positions. `expert_ids`: each row names 8 different experts; within the rows of one device (aligned blocks of 8 rows) no expert is named more than 2 times.
All inputs are finite; a program needn't handle non-finite values.
Results may differ from a plain program's by a relative error of at most 0.015.
Values may be sent and summed in bfloat16 or wider, within the bound.
A program may use at most 64 MiB of HBM per device.

v0:
```python
import math

import jax
import jax.numpy as jnp
from jax import lax
from jax.sharding import PartitionSpec as P

EXP_DEV = 4


def side_by_side(arrays, axis, dim, along):
    widths = [a.shape[along] for a in arrays]
    both = jnp.concatenate(arrays, axis=along)
    out = lax.all_gather(both, axis, axis=dim, tiled=True)
    return tuple(jnp.split(out, [sum(widths[:k]) for k in range(1, len(widths))], axis=along))


def cut_along(array, dim, peers):
    before, after = (array.shape[:dim], array.shape[dim + 1 :])
    return jnp.moveaxis(array.reshape(*before, peers, -1, *after), dim, 0)


def sent_and_summed(array, axis, dim):
    tiles = cut_along(array, dim, lax.axis_size(axis))
    arrived = lax.all_to_all(tiles, axis, split_axis=0, concat_axis=0, tiled=True)
    return arrived.astype(jnp.float32).sum(axis=0)


def grouped_exchange(array, axis, split_dim, concat_dim, work, item_dim, out_dim):

    def moved(group):
        return lax.all_to_all(group, axis, split_axis=split_dim, concat_axis=concat_dim, tiled=True)

    items = jax.tree.leaves(array)[0].shape[item_dim]
    ends = [items * k // 2 for k in range(2 + 1)] if items % 2 == 0 else [0, items]
    groups = [
        jax.tree.map(lambda a: lax.slice_in_dim(a, low, high, axis=item_dim), array)
        for low, high in zip(ends, ends[1:])
    ]
    arrived = [moved(group) for group in groups]
    made = [work(group) for group in arrived]
    return jax.tree.map(lambda *parts: jnp.concatenate(parts, axis=out_dim), *made)


def prompt_owner(places, prompt_lengths):
    prompt_ends = jnp.cumsum(prompt_lengths)
    return jnp.sum((places[:, None] >= prompt_ends[None, :-1]).astype(jnp.int32), axis=1)


def local(
    queries,
    keys,
    values,
    residual,
    prompt_lengths,
    out_proj,
    norm_gain,
    expert_ids,
    route_weights,
    w_gate,
    w_up,
    w_down,
):
    attn_count = lax.axis_size("attn")
    column_count = lax.axis_size("expert")
    attn_place = lax.axis_index("attn")
    column_place = lax.axis_index("expert")
    query_rows = queries.shape[0]
    head_size = queries.shape[1]
    query_group_count = column_count // keys.shape[0]
    kv_index = column_place // query_group_count
    own_keys = lax.dynamic_index_in_dim(keys, kv_index, 0, keepdims=False)
    own_values = lax.dynamic_index_in_dim(values, kv_index, 0, keepdims=False)
    score_scale = 1.0 / math.sqrt(head_size)
    query_places = attn_place * query_rows + jnp.arange(query_rows, dtype=jnp.int32)
    query_owner = prompt_owner(query_places, prompt_lengths)

    def absorb_block(carried, key_block, value_block, offset):
        running_max, run_total, weighted = carried
        key_places = offset + jnp.arange(key_block.shape[0], dtype=jnp.int32)
        key_owner = prompt_owner(key_places, prompt_lengths)
        visible = (key_places[None, :] <= query_places[:, None]) & (
            key_owner[None, :] == query_owner[:, None]
        )
        scores = (
            lax.dot_general(
                queries, key_block, (((1,), (1,)), ((), ())), preferred_element_type=jnp.float32
            )
            * score_scale
        )
        scores = jnp.where(visible, scores, -1e30)
        new_max = jnp.maximum(running_max, jnp.max(scores, axis=1))
        factor = jnp.exp(running_max - new_max)
        weights = jnp.where(visible, jnp.exp(scores - new_max[:, None]), 0.0)
        run_total = run_total * factor + jnp.sum(weights, axis=1)
        weighted = weighted * factor[:, None] + jnp.dot(
            weights.astype(jnp.bfloat16), value_block, preferred_element_type=jnp.float32
        )
        return (new_max, run_total, weighted)

    initial = (
        jnp.full((query_rows,), -1e30, jnp.float32),
        jnp.zeros((query_rows,), jnp.float32),
        jnp.zeros((query_rows, head_size), jnp.float32),
    )
    key_block, value_block = side_by_side((own_keys, own_values), "attn", 0, 1)
    piece_rows = key_block.shape[0]
    turns = piece_rows // 512
    key_parts = key_block.reshape(turns, 512, key_block.shape[1])
    value_parts = value_block.reshape(turns, 512, value_block.shape[1])
    starts = jnp.arange(turns, dtype=jnp.int32) * 512

    def one_turn(state, inputs):
        return (absorb_block(state, inputs[0], inputs[1], inputs[2]), None)

    folded = lax.scan(one_turn, initial, (key_parts, value_parts, starts))[0]
    attended = (folded[2] / folded[1][:, None]).astype(jnp.bfloat16)
    projected = sent_and_summed(
        jnp.dot(attended, out_proj, preferred_element_type=jnp.float32).astype(jnp.bfloat16),
        "expert",
        0,
    )
    stream = residual.astype(jnp.float32) + projected
    mean_square = jnp.mean(stream * stream, axis=1, keepdims=True)
    normalized = (stream * lax.rsqrt(mean_square + 1e-06) * norm_gain).astype(jnp.bfloat16)
    tok_rows = residual.shape[0]
    width = residual.shape[1]
    choices_per_row = expert_ids.shape[1]
    expert_total = EXP_DEV * column_count
    slot_count = max(2, 2 * tok_rows * choices_per_row // expert_total)
    labels = jnp.arange(expert_total, dtype=jnp.int32)
    matches = expert_ids[:, :, None] == labels[None, None, :]
    routed = jnp.any(matches, axis=1)
    shares = jnp.sum(jnp.where(matches, route_weights[:, :, None], 0.0), axis=1)
    counts = routed.astype(jnp.int32)
    before = jnp.cumsum(counts, axis=0) - counts
    slot_ids = jnp.arange(slot_count, dtype=jnp.int32)
    selector = routed.T[:, None, :] & (before.T[:, None, :] == slot_ids[None, :, None])
    selector = selector.reshape(expert_total * slot_count, tok_rows)
    outgoing = jnp.dot(
        selector.astype(jnp.bfloat16), normalized, preferred_element_type=jnp.float32
    ).astype(jnp.bfloat16)
    outgoing = outgoing.reshape(column_count, EXP_DEV, slot_count, width)
    arrived = lax.all_to_all(outgoing, "expert", split_axis=0, concat_axis=0, tiled=True)
    shard_count = attn_count // EXP_DEV
    spread = jnp.repeat(arrived, shard_count, axis=1)

    def run_expert(batched):
        flattened = batched.reshape(-1, batched.shape[-1])
        gate_part = jnp.dot(flattened, w_gate[0], preferred_element_type=jnp.float32)
        up_part = jnp.dot(flattened, w_up[0], preferred_element_type=jnp.float32)
        active = (jax.nn.silu(gate_part) * up_part).astype(jnp.bfloat16)
        partial_out = jnp.dot(active, w_down[0], preferred_element_type=jnp.float32).astype(
            jnp.bfloat16
        )
        return lax.all_to_all(
            partial_out.reshape(batched.shape), "attn", split_axis=1, concat_axis=1, tiled=True
        )

    returned = grouped_exchange(spread, "attn", 1, 1, run_expert, 0, 0)
    summed = jnp.sum(
        returned.reshape(column_count, EXP_DEV, shard_count, slot_count, width).astype(jnp.float32),
        axis=2,
    )
    expert_rows = lax.all_to_all(
        summed.astype(jnp.bfloat16), "expert", split_axis=0, concat_axis=0, tiled=True
    ).astype(summed.dtype)
    weighting = (
        routed.T[:, None, :].astype(jnp.float32)
        * (before.T[:, None, :] == slot_ids[None, :, None]).astype(jnp.float32)
        * shares.T[:, None, :]
    )
    weighting = weighting.reshape(expert_total * slot_count, tok_rows)
    mixed = lax.dot_general(
        weighting,
        expert_rows.reshape(expert_total * slot_count, width),
        (((0,), (0,)), ((), ())),
        preferred_element_type=jnp.float32,
    )
    return (stream + mixed).astype(jnp.bfloat16)


def solution(mesh):
    return jax.shard_map(
        local,
        mesh=mesh,
        in_specs=(
            P("attn", "expert"),
            P(None, "attn", None),
            P(None, "attn", None),
            P(("attn", "expert"), None),
            P(),
            P("expert", None),
            P(),
            P(("attn", "expert"), None),
            P(("attn", "expert"), None),
            P("expert", None, "attn"),
            P("expert", None, "attn"),
            P("expert", "attn", None),
        ),
        out_specs=P(("attn", "expert"), None),
        check_vma=False,
    )
```

profile of v0, /device:TPU:1, one launch (start us, length us, event | category | flops | bytes accessed | tf_op | source)
XLA Modules:
  0.0 442.4 jit_solution(27691235467578367)
XLA Ops:
  9.2 47.9 %all-gather.2.cloned.1.call-done = bf16[4096,256]{1,0:T(8,128)(2,1)} async-done(((bf16[256,256]{1,0:T(8,128)(2,1)}), bf16[4096,256]{1,0:T(8,128)(2,1)}) %all-gather.2.cloned.1.call-update) | async-done | bytes 2097168 | tf_op jit(solution)/shard_map/all_gather | solution.py:14
  57.1 2.7 fusion.73
  59.8 27.1 %while.17 = (s32[]{:T(128)}, f32[256]{0:T(256)S(1)}, f32[256]{0:T(256)S(1)}, f32[256,128]{1,0:T(8,128)S(1)}, s32[8]{0:T(128)S(1)}, /*index=5*/s32[4,1]{0,1:T(1,1...) while((s32[]{:T(128)}, f32[256]{0:T(256)S(1)}, ...), condition=%wide.region_6.7_spmd.clone, body=%wide.region_2.6_spmd.clone.sunk | while | flops 69572608 | bytes 2204881 | solution.py:116
  88.4 10.0 %all-to-all-start = ((bf16[32,8,2048]{2,1,0:T(8,128)(2,1)}), bf16[32,8,2048]{2,1,0:T(8,128)(2,1)S(1)}, u32[]{:S(2)}, u32[]{:S(2)}) async-start(bf16[32,8,2048]{2,1,0:T(8,128)(2,1)} %fusion.22), calls=%async_computation | async-start | bytes 2097152 | tf_op jit(solution)/shard_map/all_to_all | solution.py:25
  99.2 26.2 %all-to-all-done = bf16[32,8,2048]{2,1,0:T(8,128)(2,1)S(1)} async-done(((bf16[32,8,2048]{2,1,0:T(8,128)(2,1)}), bf16[32,8,2048]{2,1,0:T(8,128)(2,1)S(1)}, u32[]{:S(2)}, u32[]{:S(2)}) %all-to-all-start) | async-done | bytes 1048608 | tf_op jit(solution)/shard_map/all_to_all | solution.py:25
  127.7 31.4 %all_to_all.35 = bf16[32,4,2,2048]{3,2,1,0:T(2,128)(2,1)S(1)} all-to-all(bf16[32,4,2,2048]{3,2,1,0:T(2,128)(2,1)} %reshape.130), channel_id=1, replica_groups=mesh['attn'=16,'expert'=32] {'expert'}, dimensions={0} | all-to-all | bytes 2097152 | tf_op jit(solution)/shard_map/all_to_all | solution.py:144
  160.3 3.1 broadcast_in_dim.66
  163.5 7.8 %all-to-all-start.4 = ((bf16[16,16,2,2048]{3,2,0,1:T(2,128)(2,1)}), bf16[16,16,2,2048]{3,2,0,1:T(2,128)(2,1)}, u32[]{:S(2)}, u32[]{:S(2)}) async-start(bf16[16,16,2,2048]{3,2,0,1:T(2,128)(2,1)} %bitcast.84), calls=%async_computation.4 | async-start | bytes 4194304 | tf_op jit(solution)/shard_map/all_to_all | solution.py:32
  171.7 48.8 %all-to-all-done.4 = bf16[16,16,2,2048]{3,2,0,1:T(2,128)(2,1)} async-done(((bf16[16,16,2,2048]{3,2,0,1:T(2,128)(2,1)}), bf16[16,16,2,2048]{3,2,0,1:T(2,128)(2,1)}, u32[]{:S(2)}, u32[]{:S(2)}) %all-to-all-start.4) | async-done | bytes 2097184 | tf_op jit(solution)/shard_map/all_to_all | solution.py:32
  220.4 3.1 broadcast_in_dim.65
  223.5 4.8 %all-to-all-start.2 = ((bf16[16,16,2,2048]{3,2,0,1:T(2,128)(2,1)}), bf16[16,16,2,2048]{3,2,0,1:T(2,128)(2,1)}, u32[]{:S(2)}, u32[]{:S(2)}) async-start(bf16[16,16,2,2048]{3,2,0,1:T(2,128)(2,1)} %bitcast.83), calls=%async_computation.2 | async-start | bytes 4194304 | tf_op jit(solution)/shard_map/all_to_all | solution.py:32
  228.3 4.9 %copy.54 = bf16[16,16,2,2048]{3,2,1,0:T(2,128)(2,1)} copy(bf16[16,16,2,2048]{3,2,0,1:T(2,128)(2,1)} %all-to-all-done.4) | data formatting | bytes 4194304 | tf_op jit(solution)/shard_map/all_to_all | solution.py:32
  233.2 4.1 reshape.133
  237.3 3.3 fusion.30
  240.6 5.7 %convolution_convert_fusion = bf16[512,2048]{1,0:T(8,128)(2,1)} fusion(bf16[1,384,2048]{2,1,0:T(8,128)(2,1)S(1)} %copy-done, bf16[512,2048]{1,0:T(8,128)(2,1)} %reshape.133, bf16[1,2048,384]{2,1,0:T(8,128)(2,1)} %param.24, f32[512,384]{1,0:T(8,128)S(1)} %fusion.30), kind=kOutput, calls=%fused_computation.34 | convolution fusion | flops 1612840960 | bytes 8126464 | tf_op jit(solution)/shard_map/dot_general | solution.py:153
  246.4 4.4 %reshape.134 = bf16[16,16,2,2048]{3,2,1,0:T(2,128)(2,1)} reshape(bf16[512,2048]{1,0:T(8,128)(2,1)} %convolution_convert_fusion) | data formatting | bytes 4194304 | tf_op jit(solution)/shard_map/reshape | solution.py:157
  250.8 4.9 %copy.55 = bf16[16,16,2,2048]{3,2,0,1:T(2,128)(2,1)} copy(bf16[16,16,2,2048]{3,2,1,0:T(2,128)(2,1)} %reshape.134) | data formatting | bytes 4194304 | tf_op jit(solution)/shard_map/reshape | solution.py:157
  255.6 21.9 %all-to-all-done.2 = bf16[16,16,2,2048]{3,2,0,1:T(2,128)(2,1)} async-done(((bf16[16,16,2,2048]{3,2,0,1:T(2,128)(2,1)}), bf16[16,16,2,2048]{3,2,0,1:T(2,128)(2,1)}, u32[]{:S(2)}, u32[]{:S(2)}) %all-to-all-start.2) | async-done | bytes 2097184 | tf_op jit(solution)/shard_map/all_to_all | solution.py:32
  277.5 4.8 %all-to-all-start.5 = ((bf16[16,16,2,2048]{3,2,0,1:T(2,128)(2,1)}), bf16[16,16,2,2048]{3,2,0,1:T(2,128)(2,1)}, u32[]{:S(2)}, u32[]{:S(2)}) async-start(bf16[16,16,2,2048]{3,2,0,1:T(2,128)(2,1)} %copy.55), calls=%async_computation.5 | async-start | bytes 4194304 | tf_op jit(solution)/shard_map/all_to_all | solution.py:156
  282.3 4.9 %copy.51 = bf16[16,16,2,2048]{3,2,1,0:T(2,128)(2,1)} copy(bf16[16,16,2,2048]{3,2,0,1:T(2,128)(2,1)} %all-to-all-done.2) | data formatting | bytes 4194304 | tf_op jit(solution)/shard_map/all_to_all | solution.py:32
  287.2 4.1 reshape.131
  291.3 3.3 fusion.32
  294.6 5.7 %convolution_convert_fusion.1 = bf16[512,2048]{1,0:T(8,128)(2,1)} fusion(bf16[1,384,2048]{2,1,0:T(8,128)(2,1)S(1)} %copy-done, bf16[512,2048]{1,0:T(8,128)(2,1)} %reshape.131, bf16[1,2048,384]{2,1,0:T(8,128)(2,1)} %param.24, f32[512,384]{1,0:T(8,128)S(1)} %fusion.32), kind=kOutput, calls=%fused_computation.35 | convolution fusion | flops 1612840960 | bytes 8126464 | tf_op jit(solution)/shard_map/dot_general | solution.py:153
  300.3 4.4 %reshape.132 = bf16[16,16,2,2048]{3,2,1,0:T(2,128)(2,1)} reshape(bf16[512,2048]{1,0:T(8,128)(2,1)} %convolution_convert_fusion.1) | data formatting | bytes 4194304 | tf_op jit(solution)/shard_map/reshape | solution.py:157
  304.8 4.9 %copy.52 = bf16[16,16,2,2048]{3,2,0,1:T(2,128)(2,1)} copy(bf16[16,16,2,2048]{3,2,1,0:T(2,128)(2,1)} %reshape.132) | data formatting | bytes 4194304 | tf_op jit(solution)/shard_map/reshape | solution.py:157
  309.7 21.8 %all-to-all-done.5 = bf16[16,16,2,2048]{3,2,0,1:T(2,128)(2,1)} async-done(((bf16[16,16,2,2048]{3,2,0,1:T(2,128)(2,1)}), bf16[16,16,2,2048]{3,2,0,1:T(2,128)(2,1)}, u32[]{:S(2)}, u32[]{:S(2)}) %all-to-all-start.5) | async-done | bytes 2097184 | tf_op jit(solution)/shard_map/all_to_all | solution.py:156
  331.5 55.9 %all_to_all.36 = bf16[16,16,2,2048]{3,2,0,1:T(2,128)(2,1)} all-to-all(bf16[16,16,2,2048]{3,2,0,1:T(2,128)(2,1)} %copy.52), channel_id=1, replica_groups=mesh['attn'=16,'expert'=32] {'attn'}, dimensions={1} | all-to-all | bytes 4194304 | tf_op jit(solution)/shard_map/all_to_all | solution.py:156
  387.4 9.6 %bitcast_reduce_fusion = bf16[32,4,2,2048]{3,2,0,1:T(2,128)(2,1)S(1)} fusion(bf16[16,16,2,2048]{3,2,0,1:T(2,128)(2,1)} %all-to-all-done.5, bf16[16,16,2,2048]{3,2,0,1:T(2,128)(2,1)} %all_to_all.36), kind=kLoop, calls=%fused_computation.33 | loop fusion | flops 3670016 | bytes 5242880 | tf_op jit(solution)/shard_map/reduce_sum | solution.py:161
  397.0 2.1 copy.56
  399.1 5.3 %all-to-all-start.6 = ((bf16[32,4,2,2048]{3,2,1,0:T(2,128)(2,1)}), bf16[32,4,2,2048]{3,2,1,0:T(2,128)(2,1)S(1)}, u32[]{:S(2)}, u32[]{:S(2)}) async-start(bf16[32,4,2,2048]{3,2,1,0:T(2,128)(2,1)} %copy.56), calls=%async_computation.6 | async-start | bytes 2097152 | tf_op jit(solution)/shard_map/all_to_all | solution.py:165
  404.9 27.3 %all-to-all-done.6 = bf16[32,4,2,2048]{3,2,1,0:T(2,128)(2,1)S(1)} async-done(((bf16[32,4,2,2048]{3,2,1,0:T(2,128)(2,1)}), bf16[32,4,2,2048]{3,2,1,0:T(2,128)(2,1)S(1)}, u32[]{:S(2)}, u32[]{:S(2)}) %all-to-all-start.6) | async-done | bytes 1048608 | tf_op jit(solution)/shard_map/all_to_all | solution.py:165
  433.4 2.1 fusion.23
  (139 shorter events, 37.1 us)
Async XLA Ops:
  6.5 234.1 %copy-start = (bf16[1,384,2048]{2,1,0:T(8,128)(2,1)S(1)}, bf16[1,384,2048]{2,1,0:T(8,128)(2,1)}, u32[]{:S(2)}) copy-start(bf16[1,384,2048]{2,1,0:T(8,128)(2,1)} %param.25) | copy-start | bytes 4718596
  6.5 50.6 %all-gather.2.cloned.1.call-start = ((), (), s32[]{:S(2)}) async-start(), calls=%async_computation.7 | async-start | bytes 2228224 | tf_op jit(solution)/shard_map/all_gather | solution.py:14
  9.2 50.6 %copy-start.6 = (bf16[256,128]{1,0:T(8,128)(2,1)S(1)}, bf16[256,128]{1,0:T(8,128)(2,1)}, u32[]{:S(2)}) copy-start(bf16[256,128]{1,0:T(8,128)(2,1)} %param.14) | copy-start | bytes 196612
  59.8 27.2 %copy-start.1 = (bf16[128,2048]{1,0:T(8,128)(2,1)S(1)}, bf16[128,2048]{1,0:T(8,128)(2,1)}, u32[]{:S(2)}) copy-start(bf16[128,2048]{1,0:T(8,128)(2,1)} %param.19) | copy-start | bytes 1572868
  86.9 11.6 %copy-start.3 = (s32[8,8]{1,0:T(8,128)S(1)}, s32[8,8]{1,0:T(8,128)}, u32[]{:S(2)}) copy-start(s32[8,8]{1,0:T(8,128)} %param.21) | copy-start | bytes 772
  88.4 37.0 %copy-start.2 = (bf16[8,2048]{1,0:T(8,128)(2,1)S(1)}, bf16[8,2048]{1,0:T(8,128)(2,1)}, u32[]{:S(2)}) copy-start(bf16[8,2048]{1,0:T(8,128)(2,1)} %param.17) | copy-start | bytes 98308
  88.4 37.2 %copy-start.4 = (f32[2048]{0:T(1024)S(1)}, f32[2048]{0:T(1024)}, u32[]{:S(2)}) copy-start(f32[2048]{0:T(1024)} %param.20) | copy-start | bytes 24580
  88.4 36.9 %all-to-all-start = ((bf16[32,8,2048]{2,1,0:T(8,128)(2,1)}), bf16[32,8,2048]{2,1,0:T(8,128)(2,1)S(1)}, u32[]{:S(2)}, u32[]{:S(2)}) async-start(bf16[32,8,2048]{2,1,0:T(8,128)(2,1)} %fusion.22), calls=%async_computation | async-start | bytes 2097152 | tf_op jit(solution)/shard_map/all_to_all | solution.py:25
  163.5 57.0 %all-to-all-start.4 = ((bf16[16,16,2,2048]{3,2,0,1:T(2,128)(2,1)}), bf16[16,16,2,2048]{3,2,0,1:T(2,128)(2,1)}, u32[]{:S(2)}, u32[]{:S(2)}) async-start(bf16[16,16,2,2048]{3,2,0,1:T(2,128)(2,1)} %bitcast.84), calls=%async_computation.4 | async-start | bytes 4194304 | tf_op jit(solution)/shard_map/all_to_all | solution.py:32
  223.5 54.0 %all-to-all-start.2 = ((bf16[16,16,2,2048]{3,2,0,1:T(2,128)(2,1)}), bf16[16,16,2,2048]{3,2,0,1:T(2,128)(2,1)}, u32[]{:S(2)}, u32[]{:S(2)}) async-start(bf16[16,16,2,2048]{3,2,0,1:T(2,128)(2,1)} %bitcast.83), calls=%async_computation.2 | async-start | bytes 4194304 | tf_op jit(solution)/shard_map/all_to_all | solution.py:32
  277.5 54.0 %all-to-all-start.5 = ((bf16[16,16,2,2048]{3,2,0,1:T(2,128)(2,1)}), bf16[16,16,2,2048]{3,2,0,1:T(2,128)(2,1)}, u32[]{:S(2)}, u32[]{:S(2)}) async-start(bf16[16,16,2,2048]{3,2,0,1:T(2,128)(2,1)} %copy.55), calls=%async_computation.5 | async-start | bytes 4194304 | tf_op jit(solution)/shard_map/all_to_all | solution.py:156
  397.0 7.5 %copy-start.5 = (f32[8,8]{1,0:T(8,128)S(1)}, f32[8,8]{1,0:T(8,128)}, u32[]{:S(2)}) copy-start(f32[8,8]{1,0:T(8,128)} %param.22) | copy-start | bytes 772
  399.1 33.0 %all-to-all-start.6 = ((bf16[32,4,2,2048]{3,2,1,0:T(2,128)(2,1)}), bf16[32,4,2,2048]{3,2,1,0:T(2,128)(2,1)S(1)}, u32[]{:S(2)}, u32[]{:S(2)}) async-start(bf16[32,4,2,2048]{3,2,1,0:T(2,128)(2,1)} %copy.56), calls=%async_computation.6 | async-start | bytes 2097152 | tf_op jit(solution)/shard_map/all_to_all | solution.py:165
Sparse Core Ops, SparseCore 0:
  9.4 47.6 all-gather.1
where the time goes:
time: 444 us; the launch traced here: 442 us
  waiting for transfers between devices  194 us (44%)
  blocking collectives  87.3 us (20%)
  local copies, waits for them, and re-layouts  59 us (13%)
  matrix products  35.3 us (8%)
  starting transfers between devices  32.9 us (7%)
  other arithmetic  20 us (5%)
  between operations  13.6 us (3%)
    all_to_all x2, waiting for transfers between devices, moved(): lax.all_to_all(group, axis, split_axis=split_dim, concat_axis=concat_dim,...  70.6 us
    all_to_all x1, blocking collectives, run_expert(): lax.all_to_all(partial_out.reshape(batched.shape), 'attn', split_axis=1,...  55.9 us
    all_gather x1, waiting for transfers between devices, side_by_side(): out = lax.all_gather(both, axis, axis=dim, tiled=True)  47.9 us
    all_to_all x1, blocking collectives, local(): lax.all_to_all(outgoing, 'expert', split_axis=0, concat_axis=0, tiled=True)  31.4 us
    all_to_all x1, waiting for transfers between devices, local(): lax.all_to_all(summed.astype(jnp.bfloat16), 'expert', split_axis=0, conca...  27.3 us
    all_to_all x1, waiting for transfers between devices, sent_and_summed(): lax.all_to_all(tiles, axis, split_axis=0, concat_axis=0, tiled=True)  26.2 us
    all_to_all x1, waiting for transfers between devices, run_expert(): lax.all_to_all(partial_out.reshape(batched.shape), 'attn', split_axis=1,...  21.8 us
    reshape x4, local copies, waits for them, and re-layouts, run_expert(): partial_out.reshape(batched.shape)  18.6 us
  transfers between devices with their start and end apart: 6, of which 6 were waited for; matrix products, arithmetic and copies ran while one was open for 13% of the time, Pallas kernels for 0%

commit v1 on v0

v1 whole, which is shorter than its diff:
```python
import functools
import math

import jax
import jax.numpy as jnp
from jax import lax
from jax.experimental import pallas as pl
from jax.experimental.pallas import tpu as pltpu
from jax.sharding import PartitionSpec as P

BF = jnp.bfloat16
F32 = jnp.float32
VM = pltpu.VMEM
DMA = pltpu.SemaphoreType.DMA
D = 2048
DM = D + 128
RING = 8
XS = 4
QSCALE = math.log2(math.e) / math.sqrt(128.0)
ORDER = (4, 3, 5, 2, 6, 1, 7, 0)
SLOTS = (0, 1, 7, 2, 6, 3, 5, 4)


def remote(src, dst, send, recv, **dev):
    return pltpu.make_async_remote_copy(
        src_ref=src,
        dst_ref=dst,
        send_sem=send,
        recv_sem=recv,
        device_id=dev,
        device_id_type=pl.DeviceIdType.MESH,
    )


def greet(peers):
    barrier = pltpu.get_barrier_semaphore()
    for peer in peers:
        pl.semaphore_signal(barrier, inc=1, device_id=peer, device_id_type=pl.DeviceIdType.MESH)
    pl.semaphore_wait(barrier, len(peers))


def attention_kernel(
    lengths, q_ref, k_ref, v_ref, wo_ref, wg_ref, wu_ref, wd_ref,
    out_ref, pg_ref, pu_ref, pd_ref,
    kbuf, vbuf, m_ref, l_ref, acc_ref, send, recv, wsend, wrecv,
):
    a = lax.axis_index("attn")
    e = lax.axis_index("expert")
    y = a // 2
    c = a % 2
    head = e // 16
    right = ((y + 1) % RING) * 2 + c
    left = ((y + RING - 1) % RING) * 2 + c
    partner = y * 2 + (1 - c)
    greet([{"attn": right}, {"attn": left}, {"attn": partner}])
    bufs = (kbuf, vbuf)
    ins = (k_ref, v_ref)
    pending = []

    def push(kv, src, block, slot, way):
        to = (right, left, partner)[way]
        copy = remote(
            src, bufs[kv].at[block], send.at[kv, slot, way], recv.at[kv, block], attn=to
        )
        copy.start()
        pending.append(copy)

    def arrived(kv, block):
        remote(
            bufs[kv].at[block], bufs[kv].at[block], send.at[kv, 0, 0], recv.at[kv, block],
            attn=partner,
        ).wait_recv()

    wcopies = []

    def swap(step):
        for n, (mine, theirs, rows) in enumerate(
            ((wg_ref, pg_ref, 512), (wu_ref, pu_ref, 512), (wd_ref, pd_ref, 96))
        ):
            part = pl.ds(step * rows, rows)
            copy = remote(
                mine.at[0, part], theirs.at[part], wsend.at[n, step], wrecv.at[n, step],
                attn=partner,
            )
            copy.start()
            wcopies.append(copy)

    for way in (2, 0, 1):
        for kv in range(2):
            push(kv, ins[kv].at[head], a, 0, way)
    swap(0)
    kbuf[pl.ds(a, 1)] = k_ref[pl.ds(head, 1)]
    vbuf[pl.ds(a, 1)] = v_ref[pl.ds(head, 1)]

    end1 = lengths[0]
    end2 = end1 + lengths[1]
    end3 = end2 + lengths[2]
    qpos = a * 256 + lax.broadcasted_iota(jnp.int32, (256, 1), 0)
    first = jnp.where(
        qpos >= end3, end3, jnp.where(qpos >= end2, end2, jnp.where(qpos >= end1, end1, 0))
    )
    m_ref[...] = jnp.full((256, 1), -1e30, F32)
    l_ref[...] = jnp.zeros((256, 1), F32)
    acc_ref[...] = jnp.zeros((256, 128), F32)

    def attend(chunk):
        kc = kbuf[pl.ds(chunk * 2, 2)].reshape(512, 128)
        vc = vbuf[pl.ds(chunk * 2, 2)].reshape(512, 128)
        scores = lax.dot_general(
            q_ref[...], kc, (((1,), (1,)), ((), ())), preferred_element_type=F32
        )
        kpos = chunk * 512 + lax.broadcasted_iota(jnp.int32, (256, 512), 1)
        scores = jnp.where((kpos >= first) & (kpos <= qpos), scores * QSCALE, -1e30)
        old = m_ref[...]
        new = jnp.maximum(old, jnp.max(scores, axis=1, keepdims=True))
        factor = jnp.exp2(old - new)
        weights = jnp.exp2(scores - new)
        m_ref[...] = new
        l_ref[...] = l_ref[...] * factor + jnp.sum(weights, axis=1, keepdims=True)
        acc_ref[...] = acc_ref[...] * factor + jnp.dot(
            weights.astype(BF), vc, preferred_element_type=F32
        )

    for kv in range(2):
        arrived(kv, partner)
    attend(y)
    for step in range(1, 5):
        below = (y + RING - step) % RING
        above = (y + step) % RING
        if step < 4:
            for kv in range(2):
                arrived(kv, below * 2 + c)
                if step < 3 or kv == 0:
                    push(kv, bufs[kv].at[below * 2 + c], below * 2 + c, step, 0)
                push(kv, bufs[kv].at[below * 2 + c], below * 2 + c, step, 2)
            for kv in range(2):
                arrived(kv, above * 2 + c)
                if step < 3 or kv == 1:
                    push(kv, bufs[kv].at[above * 2 + c], above * 2 + c, RING - step, 1)
                push(kv, bufs[kv].at[above * 2 + c], above * 2 + c, RING - step, 2)
            swap(step)
        else:
            for kv in range(2):
                arrived(kv, below * 2 + c)
                push(kv, bufs[kv].at[below * 2 + c], below * 2 + c, 4, 2)
        for chunk in (below, above) if step < 4 else (below,):
            for kv in range(2):
                arrived(kv, chunk * 2 + (1 - c))

            @pl.when(chunk <= y)
            def _():
                attend(chunk)

    attended = (acc_ref[...] / l_ref[...]).astype(BF)
    for n in range(4):
        cols = slice(n * 512, (n + 1) * 512)
        term = jnp.dot(attended, wo_ref[:, cols], preferred_element_type=F32)
        out_ref[:, cols] = term.astype(BF)
    for copy in pending:
        copy.wait_send()
    for copy in wcopies:
        copy.wait()


def mix_heads_kernel(
    ht_ref, res_ref, gain_ref, meta_ref, stream_ref, gy_ref,
    via, fromleft, fromright, fwd, part, zin, nbuf, gbuf,
    s1, s2, s3, rvia, rleft, rright, rz, sy, ry,
):
    a = lax.axis_index("attn")
    e = lax.axis_index("expert")
    y = a // 2
    c = a % 2
    z = e // XS
    x = e % XS
    xr = (x + 1) % XS
    xl = (x + 3) % XS
    xo = (x + 2) % XS
    right = z * XS + xr
    left = z * XS + xl
    zs = [((z + r) % RING) for r in range(RING)]
    peers = [{"expert": right}, {"expert": left}]
    peers += [{"expert": zs[r] * XS + x} for r in range(1, RING)]
    ys = [((y + r) % RING) for r in range(RING)]
    peers += [{"attn": ys[r] * 2 + c} for r in range(1, RING)]
    greet(peers)
    pending = []

    def push(*args, **dev):
        copy = remote(*args, **dev)
        copy.start()
        pending.append(copy)

    def got(buf, sem):
        remote(buf, buf, sem, sem, expert=left).wait_recv()

    def block(r, col):
        return ht_ref.at[zs[r], col]

    for n, r in enumerate(ORDER):
        if n % 2 == 0:
            push(block(r, xo), via.at[r], s1.at[r, 0], rvia.at[r], expert=right)
            push(block(r, xl), fromright.at[r], s1.at[r, 1], rright.at[r], expert=left)
        else:
            push(block(r, xo), via.at[r], s1.at[r, 0], rvia.at[r], expert=left)
            push(block(r, xr), fromleft.at[r], s1.at[r, 1], rleft.at[r], expert=right)
    total = res_ref[...].astype(F32)
    for n in range(RING + 2):
        if n < RING:
            r = ORDER[n]
            got(via.at[r], rvia.at[r])
            col = xr if n % 2 == 0 else xl
            mine = ht_ref[pl.ds(zs[r], 1), pl.ds(col, 1)].reshape(8, D).astype(F32)
            fwd[r] = (via[r].astype(F32) + mine).astype(BF)
            if n % 2 == 0:
                push(fwd.at[r], fromleft.at[r], s2.at[r], rleft.at[r], expert=right)
            else:
                push(fwd.at[r], fromright.at[r], s2.at[r], rright.at[r], expert=left)
        if n >= 2:
            r = ORDER[n - 2]
            got(fromleft.at[r], rleft.at[r])
            got(fromright.at[r], rright.at[r])
            mine = ht_ref[pl.ds(zs[r], 1), pl.ds(x, 1)].reshape(8, D).astype(F32)
            summed = mine + fromleft[r].astype(F32) + fromright[r].astype(F32)
            if r == 0:
                total = total + summed
            else:
                part[r] = summed.astype(BF)
                push(part.at[r], zin.at[r], s3.at[r], rz.at[r], expert=zs[r] * XS + x)
    for r in ORDER[:-1]:
        got(zin.at[r], rz.at[r])
        total = total + zin[r].astype(F32)
    stream_ref[...] = total
    mean = jnp.mean(total * total, axis=1, keepdims=True)
    nbuf[:, :D] = (total * lax.rsqrt(mean + 1e-06) * gain_ref[...]).astype(BF)
    nbuf[:, D:] = meta_ref[...]
    gbuf[pl.ds(y, 1)] = nbuf[...].reshape(1, 8, DM)
    for r in ORDER[:-1]:
        push(nbuf, gbuf.at[y], sy.at[r], ry.at[r], attn=ys[r] * 2 + c)
    for r in range(1, RING):
        src = (y + RING - r) % RING
        got(gbuf.at[src], ry.at[r])
    for n in range(4):
        pair = gbuf[2 * n : 2 * n + 2].astype(F32).reshape(16, DM)
        gy_ref[16 * n : 16 * n + 16, :] = pair.astype(BF)
    for copy in pending:
        copy.wait_send()


def experts_kernel(
    gy_ref, stream_ref, wg_ref, wu_ref, wd_ref, pg_ref, pu_ref, pd_ref,
    out_ref,
    wg, wu, wd, toks, chosen, rows, dvia, act, outs, back, bvia, chi, clo,
    zsum, zgot, zlast, ysum, ygot,
    wsem, tsend, trecv, dsend, drecv, dvs, dvr, bsend, brecv, bvs, bvr,
    zsend, zrecv, zfin, ysend, yrecv,
):
    a = lax.axis_index("attn")
    e = lax.axis_index("expert")
    y = a // 2
    c = a % 2
    quarter = a // 4
    z = e // XS
    x = e % XS
    xr = (x + 1) % XS
    xl = (x + 3) % XS
    xo = (x + 2) % XS
    right = z * XS + xr
    left = z * XS + xl
    up = ((z + 1) % RING) * XS + x
    down = ((z + RING - 1) % RING) * XS + x
    ys = [((y + r) % RING) for r in range(RING)]
    loads = []
    for n, (src, dst) in enumerate(
        (
            (wg_ref.at[0], wg.at[:, 0:384]),
            (pg_ref, wg.at[:, 384:768]),
            (wu_ref.at[0], wu.at[:, 0:384]),
            (pu_ref, wu.at[:, 384:768]),
            (wd_ref.at[0], wd.at[0:384]),
            (pd_ref, wd.at[384:768]),
        )
    ):
        load = pltpu.make_async_copy(src, dst, wsem.at[n])
        load.start()
        loads.append(load)
    peers = [{"expert": right}, {"expert": left}, {"expert": up}, {"expert": down}]
    peers += [{"attn": ys[r] * 2 + c} for r in range(1, RING)]
    greet(peers)
    pending = []

    def push(*args, **dev):
        copy = remote(*args, **dev)
        copy.start()
        pending.append(copy)

    def got(buf, sem):
        remote(buf, buf, sem, sem, expert=left).wait_recv()

    def half(ref, slot, h):
        return ref.at[slot, pl.ds(32 * h, 32)]

    for h in range(2):
        own = gy_ref.at[pl.ds(32 * h, 32)]
        push(own, half(toks, 1, h), tsend.at[0, h, 0], trecv.at[1, h], expert=up)
        push(own, half(toks, 7, h), tsend.at[0, h, 1], trecv.at[7, h], expert=down)
    toks[0] = gy_ref[...]

    tok = lax.broadcasted_iota(jnp.int32, (64, 64), 0)
    col = lax.broadcasted_iota(jnp.int32, (64, 64), 1)
    earlier = ((tok // 8 == col // 8) & (col < tok)).astype(F32).astype(BF)
    lane = lax.broadcasted_iota(jnp.int32, (64, 128), 1)

    def choose(s):
        meta = toks[s, :, D:DM].astype(F32)
        high = pltpu.roll(meta, 120, 1)
        low = pltpu.roll(meta, 112, 1)
        hit = jnp.zeros((64, 64), F32)
        whi = jnp.zeros((64, 64), F32)
        wlo = jnp.zeros((64, 64), F32)
        for k in range(XS):
            expert = (4 * (z * XS + k) + quarter).astype(F32)
            match = (meta == expert) & (lane < 8)
            here = col // 16 == k
            hit = jnp.where(here, jnp.sum(jnp.where(match, 1.0, 0.0), 1, keepdims=True), hit)
            whi = jnp.where(here, jnp.sum(jnp.where(match, high, 0.0), 1, keepdims=True), whi)
            wlo = jnp.where(here, jnp.sum(jnp.where(match, low, 0.0), 1, keepdims=True), wlo)
        before = jnp.dot(earlier, hit.astype(BF), preferred_element_type=F32)
        place = (2 * (tok // 8)).astype(F32) + before
        pick = jnp.where((col % 16).astype(F32) == place, hit, 0.0)
        chi[s] = (pick * whi).astype(BF)
        clo[s] = (pick * wlo).astype(BF)
        pick = pick.astype(BF)
        for n in range(4):
            cols = slice(n * 512, (n + 1) * 512)
            got_rows = lax.dot_general(
                pick, toks[s, :, cols], (((0,), (0,)), ((), ())), preferred_element_type=F32
            )
            chosen[s, :, :, cols] = got_rows.astype(BF).reshape(XS, 16, 512)

    def ffn(s):
        block = rows[s].reshape(64, D)
        for n in range(3):
            cols = slice(n * 256, (n + 1) * 256)
            gate = jnp.dot(block, wg[:, cols], preferred_element_type=F32)
            lift = jnp.dot(block, wu[:, cols], preferred_element_type=F32)
            act[:, cols] = (gate / (1.0 + jnp.exp(-gate)) * lift).astype(BF)
        for n in range(4):
            cols = slice(n * 512, (n + 1) * 512)
            made = jnp.dot(act[...], wd[:, cols], preferred_element_type=F32)
            outs[s, :, :, cols] = made.astype(BF).reshape(XS, 16, 512)

    def spread(s, src, dst, via, ss, rr, vr):
        push(src.at[s, xr], dst.at[s, x], ss.at[s, 0], rr.at[s, x], expert=right)
        push(src.at[s, xl], dst.at[s, x], ss.at[s, 1], rr.at[s, x], expert=left)
        push(
            src.at[s, xo], via.at[s], ss.at[s, 2], vr.at[s],
            expert=right if SLOTS.index(s) % 2 == 0 else left,
        )

    def relay(s, dst, via, vs, rr, vr):
        got(via.at[s], vr.at[s])
        if SLOTS.index(s) % 2 == 0:
            push(via.at[s], dst.at[s, xl], vs.at[s], rr.at[s, xl], expert=right)
        else:
            push(via.at[s], dst.at[s, xr], vs.at[s], rr.at[s, xr], expert=left)

    for n in range(RING + 3):
        if n < RING:
            s = SLOTS[n]
            if s:
                for h in range(2):
                    got(half(toks, s, h), trecv.at[s, h])
                    if s < 3 or (s == 3 and h == 0):
                        push(
                            half(toks, s, h), half(toks, s + 1, h), tsend.at[s, h, 0],
                            trecv.at[s + 1, h], expert=up,
                        )
                    if s > 5 or (s == 5 and h == 1):
                        push(
                            half(toks, s, h), half(toks, s - 1, h), tsend.at[s, h, 1],
                            trecv.at[s - 1, h], expert=down,
                        )
            choose(s)
            spread(s, chosen, rows, dvia, dsend, drecv, dvr)
            rows[s, pl.ds(x, 1)] = chosen[s, pl.ds(x, 1)]
        if 1 <= n < RING + 1:
            relay(SLOTS[n - 1], rows, dvia, dvs, drecv, dvr)
        if 2 <= n < RING + 2:
            s = SLOTS[n - 2]
            for k in (xl, xr, xo):
                got(rows.at[s, k], drecv.at[s, k])
            if n == 2:
                for load in loads:
                    load.wait()
            ffn(s)
            spread(s, outs, back, bvia, bsend, brecv, bvr)
            back[s, pl.ds(x, 1)] = outs[s, pl.ds(x, 1)]
        if 3 <= n:
            relay(SLOTS[n - 3], back, bvia, bvs, brecv, bvr)

    def combine(s, h):
        part = slice(32 * h, 32 * h + 32)
        made = back[s].reshape(64, D)
        return jnp.dot(chi[s, part, :], made, preferred_element_type=F32) + jnp.dot(
            clo[s, part, :], made, preferred_element_type=F32
        )

    for s in reversed(SLOTS):
        for k in (xl, xr, xo):
            got(back.at[s, k], brecv.at[s, k])
        for h in range(2):
            value = combine(s, h)
            part = slice(32 * h, 32 * h + 32)
            if s == 0:
                for way in range(2):
                    got(zlast.at[way, pl.ds(32 * h, 32)], zfin.at[way, h])
                    value = value + zlast[way, part, :].astype(F32)
                for j in range(4):
                    row = 4 * h + j
                    ysum[row] = value[8 * j : 8 * j + 8].astype(BF)
                continue
            if s in (1, 2, 6, 7) or (s == 3 and h == 0) or (s == 5 and h == 1):
                got(half(zgot, s, h), zrecv.at[s, h])
                value = value + zgot[s, part, :].astype(F32)
            zsum[s, part, :] = value.astype(BF)
            downward = s < 4 or (s == 4 and h == 0)
            to = s - 1 if downward else (s + 1) % RING
            if to == 0:
                way = 0 if downward else 1
                push(
                    half(zsum, s, h), zlast.at[way, pl.ds(32 * h, 32)], zsend.at[s, h],
                    zfin.at[way, h], expert=down if downward else up,
                )
            else:
                push(
                    half(zsum, s, h), half(zgot, to, h), zsend.at[s, h], zrecv.at[to, h],
                    expert=down if downward else up,
                )
    for r in ORDER[:-1]:
        push(ysum.at[ys[r]], ygot.at[r], ysend.at[r], yrecv.at[r], attn=ys[r] * 2 + c)
    total = stream_ref[...] + ysum[pl.ds(y, 1)].reshape(8, D).astype(F32)
    for r in range(1, RING):
        got(ygot.at[r], yrecv.at[r])
        total = total + ygot[r].astype(F32)
    out_ref[...] = total.astype(BF)
    for copy in pending:
        copy.wait_send()


def vmem(*shape, dtype=BF):
    return VM(shape, dtype)


def local(
    queries, keys, values, residual, prompt_lengths, out_proj, norm_gain,
    expert_ids, route_weights, w_gate, w_up, w_down,
):
    inv = pl.BlockSpec(memory_space=VM)
    anyw = pl.BlockSpec(memory_space=pl.ANY)
    smem = pl.BlockSpec(memory_space=pltpu.SMEM)
    high = lax.reduce_precision(route_weights, 8, 7)
    low = route_weights - high
    meta = jnp.concatenate(
        [expert_ids.astype(F32), high, low, jnp.zeros((8, 104), F32)], axis=1
    ).astype(BF)

    terms, pg, pu, pd = pl.pallas_call(
        attention_kernel,
        out_shape=(
            jax.ShapeDtypeStruct((256, D), BF),
            jax.ShapeDtypeStruct((D, 384), BF),
            jax.ShapeDtypeStruct((D, 384), BF),
            jax.ShapeDtypeStruct((384, D), BF),
        ),
        in_specs=[smem, inv, inv, inv, inv, anyw, anyw, anyw],
        out_specs=(inv, anyw, anyw, anyw),
        scratch_shapes=[
            vmem(16, 256, 128),
            vmem(16, 256, 128),
            vmem(256, 1, dtype=F32),
            vmem(256, 1, dtype=F32),
            vmem(256, 128, dtype=F32),
            DMA((2, 8, 3)),
            DMA((2, 16)),
            DMA((3, 4)),
            DMA((3, 4)),
        ],
        compiler_params=pltpu.CompilerParams(collective_id=0, has_side_effects=True),
        name="attention",
    )(prompt_lengths, queries, keys, values, out_proj, w_gate, w_up, w_down)

    stream, rows = pl.pallas_call(
        mix_heads_kernel,
        out_shape=(jax.ShapeDtypeStruct((8, D), F32), jax.ShapeDtypeStruct((64, DM), BF)),
        in_specs=[inv] * 4,
        out_specs=(inv, inv),
        scratch_shapes=[vmem(8, 8, D)] * 6
        + [vmem(8, DM), vmem(8, 8, DM)]
        + [DMA((8, 2))]
        + [DMA((8,))] * 8,
        compiler_params=pltpu.CompilerParams(collective_id=1, has_side_effects=True),
        name="mix_heads",
    )(terms.reshape(8, 4, 8, D), residual, norm_gain.reshape(1, D), meta)

    return pl.pallas_call(
        experts_kernel,
        out_shape=jax.ShapeDtypeStruct((8, D), BF),
        in_specs=[inv, inv] + [anyw] * 6,
        out_specs=inv,
        scratch_shapes=[
            vmem(D, 768),
            vmem(D, 768),
            vmem(768, D),
            vmem(8, 64, DM),
            vmem(8, 4, 16, D),
            vmem(8, 4, 16, D),
            vmem(8, 16, D),
            vmem(64, 768),
            vmem(8, 4, 16, D),
            vmem(8, 4, 16, D),
            vmem(8, 16, D),
            vmem(8, 64, 64),
            vmem(8, 64, 64),
            vmem(8, 64, D),
            vmem(8, 64, D),
            vmem(2, 64, D),
            vmem(8, 8, D),
            vmem(8, 8, D),
            DMA((6,)),
            DMA((8, 2, 2)),
            DMA((8, 2)),
            DMA((8, 3)),
            DMA((8, 4)),
            DMA((8,)),
            DMA((8,)),
            DMA((8, 3)),
            DMA((8, 4)),
            DMA((8,)),
            DMA((8,)),
            DMA((8, 2)),
            DMA((8, 2)),
            DMA((2, 2)),
            DMA((8,)),
            DMA((8,)),
        ],
        compiler_params=pltpu.CompilerParams(collective_id=2, has_side_effects=True),
        name="experts",
    )(rows, stream, w_gate, w_up, w_down, pg, pu, pd)


def solution(mesh):
    return jax.shard_map(
        local,
        mesh=mesh,
        in_specs=(
            P("attn", "expert"),
            P(None, "attn", None),
            P(None, "attn", None),
            P(("attn", "expert"), None),
            P(),
            P("expert", None),
            P(),
            P(("attn", "expert"), None),
            P(("attn", "expert"), None),
            P("expert", None, "attn"),
            P("expert", None, "attn"),
            P("expert", "attn", None),
        ),
        out_specs=P(("attn", "expert"), None),
        check_vma=False,
    )
```

time: 444 us -> 163 us (0.37)
  the two profiles are of different devices: /device:TPU:1 before, /device:TPU:2 now
where the time goes in v1:
time: 163 us; the launch traced here: 162 us
  Pallas kernels  159 us (98%)
  other arithmetic  2.04 us (1%)
    pallas_call x1, Pallas kernels, local(): pl.pallas_call(experts_kernel, out_shape=jax.ShapeDtypeStruct((8, D), BF)...  94.6 us
    pallas_call x1, Pallas kernels, local(): pl.pallas_call(mix_heads_kernel, out_shape=(jax.ShapeDtypeStruct((8, D),...  39.7 us
    pallas_call x1, Pallas kernels, local(): pl.pallas_call(attention_kernel, out_shape=(jax.ShapeDtypeStruct((256, D)...  24.3 us

profile of v1, /device:TPU:2, one launch (start us, length us, event | category | flops | bytes accessed | tf_op | source)
XLA Modules:
  0.0 162.1 jit_solution(2804333678670495938)
XLA Ops:
  0.0 0.1 pad.3.clone
  0.1 0.7 convert_convert_fusion
  0.8 0.7 reduce-precision_convert_fusion
  1.5 0.7 maximum_maximum_fusion.meta_ref
  2.1 24.3 %attention.1 = (bf16[256,2048]{1,0:T(8,128)(2,1)}, bf16[2048,384]{1,0:T(8,128)(2,1)}, bf16[2048,384]{1,0:T(8,128)(2,1)}, bf16[384,2048]{1,0:T(8,128)(2,1)}) custom-call(s32[4]{0:T(128)} %lengths.1, bf16[256,128]{1,0:T(8,128)(2,1)} %q_ref.1, bf16[2,256,128]{2,1,0:T(8,128)(2,1)} %k_ref.1, bf16[2,256,128]{2,1,0:T(8,128)(2,1)} %v_ref.1, ...), custom_call_target="tpu_custom_call" | custom-call | tf_op jit(solution)/shard_map/attention/pallas_call | solution.py:468
  26.4 39.7 %mix_heads.1 = (f32[8,2048]{1,0:T(8,128)}, bf16[64,2176]{1,0:T(8,128)(2,1)}) custom-call(bf16[8,4,8,2048]{3,2,1,0:T(8,128)(2,1)} %bitcast.2, bf16[8,2048]{1,0:T(8,128)(2,1)} %res_ref.1, f32[1,2048]{1,0:T(1,128)} %bitcast.3, bf16[8,128]{1,0:T(8,128)(2,1)} %maximum_maximum_fusion.meta_ref), custom_call_target="tpu_custom_call" | custom-call | tf_op jit(solution)/shard_map/mix_heads/pallas_call | solution.py:493
  66.1 94.6 %experts.1 = bf16[8,2048]{1,0:T(8,128)(2,1)} custom-call(bf16[64,2176]{1,0:T(8,128)(2,1)} %get-tuple-element.12.gy_ref, f32[8,2048]{1,0:T(8,128)} %get-tuple-element.13.stream_ref, bf16[1,2048,384]{2,1,0:T(8,128)(2,1)} %wg_ref.3, bf16[1,2048,384]{2,1,0:T(8,128)(2,1)} %wu_ref.3, bf16[1,384,2048]{2,1,0:T(8,128)(2,1)} %wd_ref.3, ...), custom_call_target="tpu_custom_call" | custom-call | tf_op jit(solution)/shard_map/experts/pallas_call | solution.py:506
  160.8 1.4 copy.14
  (1 shorter events, 0.0 us)

commit v2 on v1

--- a/solution.py
+++ b/solution.py
@@ -1,4 +1,3 @@
-import functools
 import math
 
 import jax
@@ -13,7 +12,10 @@
 VM = pltpu.VMEM
 DMA = pltpu.SemaphoreType.DMA
 D = 2048
-DM = D + 128
+EX = 640
+W = D - EX
+TW = W + 128
+CUTS = ((0, 512), (512, 1024), (1024, W))
 RING = 8
 XS = 4
 QSCALE = math.log2(math.e) / math.sqrt(128.0)
@@ -164,8 +166,8 @@
 
 def mix_heads_kernel(
     ht_ref, res_ref, gain_ref, meta_ref, stream_ref, gy_ref,
-    via, fromleft, fromright, fwd, part, zin, nbuf, gbuf,
-    s1, s2, s3, rvia, rleft, rright, rz, sy, ry,
+    xin, part, zin, nbuf, gbuf,
+    s1, s3, rx, rz, sy, ry,
 ):
     a = lax.axis_index("attn")
     e = lax.axis_index("expert")
@@ -173,15 +175,11 @@
     c = a % 2
     z = e // XS
     x = e % XS
-    xr = (x + 1) % XS
-    xl = (x + 3) % XS
-    xo = (x + 2) % XS
-    right = z * XS + xr
-    left = z * XS + xl
+    xs = [(x + d) % XS for d in range(XS)]
     zs = [((z + r) % RING) for r in range(RING)]
-    peers = [{"expert": right}, {"expert": left}]
+    ys = [((y + r) % RING) for r in range(RING)]
+    peers = [{"expert": z * XS + xs[d]} for d in range(1, XS)]
     peers += [{"expert": zs[r] * XS + x} for r in range(1, RING)]
-    ys = [((y + r) % RING) for r in range(RING)]
     peers += [{"attn": ys[r] * 2 + c} for r in range(1, RING)]
     greet(peers)
     pending = []
@@ -192,56 +190,42 @@
         pending.append(copy)
 
     def got(buf, sem):
-        remote(buf, buf, sem, sem, expert=left).wait_recv()
-
-    def block(r, col):
-        return ht_ref.at[zs[r], col]
-
-    for n, r in enumerate(ORDER):
-        if n % 2 == 0:
-            push(block(r, xo), via.at[r], s1.at[r, 0], rvia.at[r], expert=right)
-            push(block(r, xl), fromright.at[r], s1.at[r, 1], rright.at[r], expert=left)
+        remote(buf, buf, sem, sem, expert=z * XS + xs[1]).wait_recv()
+
+    for r in ORDER:
+        for d in (2, 1, 3):
+            push(
+                ht_ref.at[zs[r], xs[d]], xin.at[r, d - 1], s1.at[r, d - 1], rx.at[r, d - 1],
+                expert=z * XS + xs[d],
+            )
+    total = res_ref[...].astype(F32)
+    for r in ORDER:
+        summed = ht_ref[pl.ds(zs[r], 1), pl.ds(x, 1)].reshape(8, D).astype(F32)
+        for d in range(XS - 1):
+            got(xin.at[r, d], rx.at[r, d])
+            summed = summed + xin[r, d].astype(F32)
+        if r == 0:
+            total = total + summed
         else:
-            push(block(r, xo), via.at[r], s1.at[r, 0], rvia.at[r], expert=left)
-            push(block(r, xr), fromleft.at[r], s1.at[r, 1], rleft.at[r], expert=right)
-    total = res_ref[...].astype(F32)
-    for n in range(RING + 2):
-        if n < RING:
-            r = ORDER[n]
-            got(via.at[r], rvia.at[r])
-            col = xr if n % 2 == 0 else xl
-            mine = ht_ref[pl.ds(zs[r], 1), pl.ds(col, 1)].reshape(8, D).astype(F32)
-            fwd[r] = (via[r].astype(F32) + mine).astype(BF)
-            if n % 2 == 0:
-                push(fwd.at[r], fromleft.at[r], s2.at[r], rleft.at[r], expert=right)
-            else:
-                push(fwd.at[r], fromright.at[r], s2.at[r], rright.at[r], expert=left)
-        if n >= 2:
-            r = ORDER[n - 2]
-            got(fromleft.at[r], rleft.at[r])
-            got(fromright.at[r], rright.at[r])
-            mine = ht_ref[pl.ds(zs[r], 1), pl.ds(x, 1)].reshape(8, D).astype(F32)
-            summed = mine + fromleft[r].astype(F32) + fromright[r].astype(F32)
-            if r == 0:
-                total = total + summed
-            else:
-                part[r] = summed.astype(BF)
-                push(part.at[r], zin.at[r], s3.at[r], rz.at[r], expert=zs[r] * XS + x)
+            part[r] = summed.astype(BF)
+            push(part.at[r], zin.at[r], s3.at[r], rz.at[r], expert=zs[r] * XS + x)
     for r in ORDER[:-1]:
         got(zin.at[r], rz.at[r])
         total = total + zin[r].astype(F32)
+    mean = jnp.mean(total * total, axis=1, keepdims=True)
+    normalized = (total * lax.rsqrt(mean + 1e-06) * gain_ref[...]).astype(BF)
+    for p in range(2):
+        nbuf[p, :, :W] = normalized[:, p * EX : p * EX + W]
+        nbuf[p, :, W:] = meta_ref[...]
+    for r in ORDER[:-1]:
+        push(nbuf.at[ys[r] % 2], gbuf.at[y], sy.at[r], ry.at[r], attn=ys[r] * 2 + c)
     stream_ref[...] = total
-    mean = jnp.mean(total * total, axis=1, keepdims=True)
-    nbuf[:, :D] = (total * lax.rsqrt(mean + 1e-06) * gain_ref[...]).astype(BF)
-    nbuf[:, D:] = meta_ref[...]
-    gbuf[pl.ds(y, 1)] = nbuf[...].reshape(1, 8, DM)
-    for r in ORDER[:-1]:
-        push(nbuf, gbuf.at[y], sy.at[r], ry.at[r], attn=ys[r] * 2 + c)
+    gbuf[pl.ds(y, 1)] = nbuf[pl.ds(y % 2, 1)]
     for r in range(1, RING):
         src = (y + RING - r) % RING
         got(gbuf.at[src], ry.at[r])
     for n in range(4):
-        pair = gbuf[2 * n : 2 * n + 2].astype(F32).reshape(16, DM)
+        pair = gbuf[2 * n : 2 * n + 2].astype(F32).reshape(16, TW)
         gy_ref[16 * n : 16 * n + 16, :] = pair.astype(BF)
     for copy in pending:
         copy.wait_send()
@@ -250,41 +234,49 @@
 def experts_kernel(
     gy_ref, stream_ref, wg_ref, wu_ref, wd_ref, pg_ref, pu_ref, pd_ref,
     out_ref,
-    wg, wu, wd, toks, chosen, rows, dvia, act, outs, back, bvia, chi, clo,
+    wg, wu, wd, toks, chosen, rows, mrows, act, outs, mouts, madd, fine, back, chi, clo,
     zsum, zgot, zlast, ysum, ygot,
-    wsem, tsend, trecv, dsend, drecv, dvs, dvr, bsend, brecv, bvs, bvr,
+    wsem, tsend, trecv, dsend, drecv, msend, mrecv, nsend, nrecv, bsend, brecv,
     zsend, zrecv, zfin, ysend, yrecv,
 ):
     a = lax.axis_index("attn")
     e = lax.axis_index("expert")
     y = a // 2
     c = a % 2
+    odd = y % 2
     quarter = a // 4
     z = e // XS
     x = e % XS
-    xr = (x + 1) % XS
-    xl = (x + 3) % XS
-    xo = (x + 2) % XS
-    right = z * XS + xr
-    left = z * XS + xl
+    xs = [(x + d) % XS for d in range(XS)]
     up = ((z + 1) % RING) * XS + x
     down = ((z + RING - 1) % RING) * XS + x
     ys = [((y + r) % RING) for r in range(RING)]
+    mate = (y + 1 - 2 * odd) * 2 + c
+    own_cols = pl.ds(pl.multiple_of(odd * EX, 128), W)
+    mate_cols = pl.ds(pl.multiple_of((1 - odd) * W, 128), EX)
+    shared = pl.ds(pl.multiple_of(odd * (W - EX), 128), EX)
     loads = []
-    for n, (src, dst) in enumerate(
-        (
-            (wg_ref.at[0], wg.at[:, 0:384]),
-            (pg_ref, wg.at[:, 384:768]),
-            (wu_ref.at[0], wu.at[:, 0:384]),
-            (pu_ref, wu.at[:, 384:768]),
-            (wd_ref.at[0], wd.at[0:384]),
-            (pd_ref, wd.at[384:768]),
-        )
+    for n, (mine, theirs, dst) in enumerate(
+        ((wg_ref.at[0], pg_ref, wg), (wu_ref.at[0], pu_ref, wu), (wd_ref.at[0], pd_ref, wd))
     ):
-        load = pltpu.make_async_copy(src, dst, wsem.at[n])
-        load.start()
-        loads.append(load)
-    peers = [{"expert": right}, {"expert": left}, {"expert": up}, {"expert": down}]
+        for k, src in enumerate((mine, theirs)):
+            span = pl.ds(384 * k, 384)
+            if n < 2:
+                pairs = (
+                    (src.at[own_cols], dst.at[pl.ds(0, W), span]),
+                    (src.at[mate_cols], dst.at[pl.ds(W, EX), span]),
+                )
+            else:
+                pairs = (
+                    (src.at[:, own_cols], dst.at[span, pl.ds(0, W)]),
+                    (src.at[:, mate_cols], dst.at[span, pl.ds(W, EX)]),
+                )
+            for i, (from_ref, to_ref) in enumerate(pairs):
+                load = pltpu.make_async_copy(from_ref, to_ref, wsem.at[4 * n + 2 * k + i])
+                load.start()
+                loads.append(load)
+    peers = [{"expert": z * XS + xs[d]} for d in range(1, XS)]
+    peers += [{"expert": up}, {"expert": down}]
     peers += [{"attn": ys[r] * 2 + c} for r in range(1, RING)]
     greet(peers)
     pending = []
@@ -295,7 +287,7 @@
         pending.append(copy)
 
     def got(buf, sem):
-        remote(buf, buf, sem, sem, expert=left).wait_recv()
+        remote(buf, buf, sem, sem, expert=up).wait_recv()
 
     def half(ref, slot, h):
         return ref.at[slot, pl.ds(32 * h, 32)]
@@ -312,7 +304,7 @@
     lane = lax.broadcasted_iota(jnp.int32, (64, 128), 1)
 
     def choose(s):
-        meta = toks[s, :, D:DM].astype(F32)
+        meta = toks[s, :, W:TW].astype(F32)
         high = pltpu.roll(meta, 120, 1)
         low = pltpu.roll(meta, 112, 1)
         hit = jnp.zeros((64, 64), F32)
@@ -331,41 +323,43 @@
         chi[s] = (pick * whi).astype(BF)
         clo[s] = (pick * wlo).astype(BF)
         pick = pick.astype(BF)
-        for n in range(4):
-            cols = slice(n * 512, (n + 1) * 512)
+        for lo, hi in CUTS:
             got_rows = lax.dot_general(
-                pick, toks[s, :, cols], (((0,), (0,)), ((), ())), preferred_element_type=F32
+                pick, toks[s, :, lo:hi], (((0,), (0,)), ((), ())), preferred_element_type=F32
             )
-            chosen[s, :, :, cols] = got_rows.astype(BF).reshape(XS, 16, 512)
+            chosen[s, :, :, lo:hi] = got_rows.astype(BF).reshape(XS, 16, hi - lo)
 
     def ffn(s):
-        block = rows[s].reshape(64, D)
+        block = rows[s].reshape(64, W)
+        rest = mrows[s].reshape(64, EX)
         for n in range(3):
             cols = slice(n * 256, (n + 1) * 256)
-            gate = jnp.dot(block, wg[:, cols], preferred_element_type=F32)
-            lift = jnp.dot(block, wu[:, cols], preferred_element_type=F32)
+            gate = jnp.dot(block, wg[:W, cols], preferred_element_type=F32) + jnp.dot(
+                rest, wg[W:, cols], preferred_element_type=F32
+            )
+            lift = jnp.dot(block, wu[:W, cols], preferred_element_type=F32) + jnp.dot(
+                rest, wu[W:, cols], preferred_element_type=F32
+            )
             act[:, cols] = (gate / (1.0 + jnp.exp(-gate)) * lift).astype(BF)
-        for n in range(4):
-            cols = slice(n * 512, (n + 1) * 512)
-            made = jnp.dot(act[...], wd[:, cols], preferred_element_type=F32)
-            outs[s, :, :, cols] = made.astype(BF).reshape(XS, 16, 512)
-
-    def spread(s, src, dst, via, ss, rr, vr):
-        push(src.at[s, xr], dst.at[s, x], ss.at[s, 0], rr.at[s, x], expert=right)
-        push(src.at[s, xl], dst.at[s, x], ss.at[s, 1], rr.at[s, x], expert=left)
-        push(
-            src.at[s, xo], via.at[s], ss.at[s, 2], vr.at[s],
-            expert=right if SLOTS.index(s) % 2 == 0 else left,
-        )
-
-    def relay(s, dst, via, vs, rr, vr):
-        got(via.at[s], vr.at[s])
-        if SLOTS.index(s) % 2 == 0:
-            push(via.at[s], dst.at[s, xl], vs.at[s], rr.at[s, xl], expert=right)
-        else:
-            push(via.at[s], dst.at[s, xr], vs.at[s], rr.at[s, xr], expert=left)
-
-    for n in range(RING + 3):
+        made = jnp.dot(act[...], wd[:, W:], preferred_element_type=F32)
+        mouts[s] = made.astype(BF).reshape(XS, 16, EX)
+        push(mouts.at[s], madd.at[s], nsend.at[s], nrecv.at[s], attn=mate)
+        for lo, hi in CUTS:
+            made = jnp.dot(act[...], wd[:, lo:hi], preferred_element_type=F32)
+            fine[s, :, lo:hi] = made
+
+    def spread(s, src, dst, ss, rr):
+        for d in (2, 1, 3):
+            push(
+                src.at[s, xs[d]], dst.at[s, x], ss.at[s, d - 1], rr.at[s, x],
+                expert=z * XS + xs[d],
+            )
+
+    def gathered(s, buf, rr):
+        for d in (1, 3, 2):
+            got(buf.at[s, xs[d]], rr.at[s, xs[d]])
+
+    for n in range(RING + 6):
         if n < RING:
             s = SLOTS[n]
             if s:
@@ -382,33 +376,36 @@
                             trecv.at[s - 1, h], expert=down,
                         )
             choose(s)
-            spread(s, chosen, rows, dvia, dsend, drecv, dvr)
+            spread(s, chosen, rows, dsend, drecv)
             rows[s, pl.ds(x, 1)] = chosen[s, pl.ds(x, 1)]
-        if 1 <= n < RING + 1:
-            relay(SLOTS[n - 1], rows, dvia, dvs, drecv, dvr)
         if 2 <= n < RING + 2:
             s = SLOTS[n - 2]
-            for k in (xl, xr, xo):
-                got(rows.at[s, k], drecv.at[s, k])
-            if n == 2:
+            gathered(s, rows, drecv)
+            push(rows.at[s, :, :, shared], mrows.at[s], msend.at[s], mrecv.at[s], attn=mate)
+        if 4 <= n < RING + 4:
+            s = SLOTS[n - 4]
+            got(mrows.at[s], mrecv.at[s])
+            if n == 4:
                 for load in loads:
                     load.wait()
             ffn(s)
-            spread(s, outs, back, bvia, bsend, brecv, bvr)
+        if 6 <= n:
+            s = SLOTS[n - 6]
+            got(madd.at[s], nrecv.at[s])
+            fine[s, :, shared] = fine[s, :, shared] + madd[s].reshape(64, EX).astype(F32)
+            outs[s] = fine[s].astype(BF).reshape(XS, 16, W)
+            spread(s, outs, back, bsend, brecv)
             back[s, pl.ds(x, 1)] = outs[s, pl.ds(x, 1)]
-        if 3 <= n:
-            relay(SLOTS[n - 3], back, bvia, bvs, brecv, bvr)
 
     def combine(s, h):
         part = slice(32 * h, 32 * h + 32)
-        made = back[s].reshape(64, D)
+        made = back[s].reshape(64, W)
         return jnp.dot(chi[s, part, :], made, preferred_element_type=F32) + jnp.dot(
             clo[s, part, :], made, preferred_element_type=F32
         )
 
     for s in reversed(SLOTS):
-        for k in (xl, xr, xo):
-            got(back.at[s, k], brecv.at[s, k])
+        gathered(s, back, brecv)
         for h in range(2):
             value = combine(s, h)
             part = slice(32 * h, 32 * h + 32)
@@ -439,11 +436,19 @@
                 )
     for r in ORDER[:-1]:
         push(ysum.at[ys[r]], ygot.at[r], ysend.at[r], yrecv.at[r], attn=ys[r] * 2 + c)
-    total = stream_ref[...] + ysum[pl.ds(y, 1)].reshape(8, D).astype(F32)
+    same = ysum[pl.ds(y, 1)].reshape(8, W).astype(F32)
+    other = jnp.zeros((8, W), F32)
     for r in range(1, RING):
         got(ygot.at[r], yrecv.at[r])
-        total = total + ygot[r].astype(F32)
-    out_ref[...] = total.astype(BF)
+        if r % 2 == 0:
+            same = same + ygot[r].astype(F32)
+        else:
+            other = other + ygot[r].astype(F32)
+    evens = jnp.where(odd == 0, same, other)
+    odds = jnp.where(odd == 0, other, same)
+    out_ref[:, :EX] = (stream_ref[:, :EX] + evens[:, :EX]).astype(BF)
+    out_ref[:, EX:W] = (stream_ref[:, EX:W] + evens[:, EX:] + odds[:, : W - EX]).astype(BF)
+    out_ref[:, W:] = (stream_ref[:, W:] + odds[:, W - EX :]).astype(BF)
     for copy in pending:
         copy.wait_send()
 
@@ -492,13 +497,12 @@
 
     stream, rows = pl.pallas_call(
         mix_heads_kernel,
-        out_shape=(jax.ShapeDtypeStruct((8, D), F32), jax.ShapeDtypeStruct((64, DM), BF)),
+        out_shape=(jax.ShapeDtypeStruct((8, D), F32), jax.ShapeDtypeStruct((64, TW), BF)),
         in_specs=[inv] * 4,
         out_specs=(inv, inv),
-        scratch_shapes=[vmem(8, 8, D)] * 6
-        + [vmem(8, DM), vmem(8, 8, DM)]
-        + [DMA((8, 2))]
-        + [DMA((8,))] * 8,
+        scratch_shapes=[vmem(8, 3, 8, D), vmem(8, 8, D), vmem(8, 8, D)]
+        + [vmem(2, 8, TW), vmem(8, 8, TW)]
+        + [DMA((8, 3)), DMA((8,)), DMA((8, 3)), DMA((8,)), DMA((8,)), DMA((8,))],
         compiler_params=pltpu.CompilerParams(collective_id=1, has_side_effects=True),
         name="mix_heads",
     )(terms.reshape(8, 4, 8, D), residual, norm_gain.reshape(1, D), meta)
@@ -512,32 +516,34 @@
             vmem(D, 768),
             vmem(D, 768),
             vmem(768, D),
-            vmem(8, 64, DM),
-            vmem(8, 4, 16, D),
-            vmem(8, 4, 16, D),
-            vmem(8, 16, D),
+            vmem(8, 64, TW),
+            vmem(8, 4, 16, W),
+            vmem(8, 4, 16, W),
+            vmem(8, 4, 16, EX),
             vmem(64, 768),
-            vmem(8, 4, 16, D),
-            vmem(8, 4, 16, D),
-            vmem(8, 16, D),
+            vmem(8, 4, 16, W),
+            vmem(8, 4, 16, EX),
+            vmem(8, 4, 16, EX),
+            vmem(8, 64, W, dtype=F32),
+            vmem(8, 4, 16, W),
             vmem(8, 64, 64),
             vmem(8, 64, 64),
-            vmem(8, 64, D),
-            vmem(8, 64, D),
-            vmem(2, 64, D),
-            vmem(8, 8, D),
-            vmem(8, 8, D),
-            DMA((6,)),
+            vmem(8, 64, W),
+            vmem(8, 64, W),
+            vmem(2, 64, W),
+            vmem(8, 8, W),
+            vmem(8, 8, W),
+            DMA((12,)),
             DMA((8, 2, 2)),
             DMA((8, 2)),
             DMA((8, 3)),
             DMA((8, 4)),
             DMA((8,)),
             DMA((8,)),
+            DMA((8,)),
+            DMA((8,)),
             DMA((8, 3)),
             DMA((8, 4)),
-            DMA((8,)),
-            DMA((8,)),
             DMA((8, 2)),
             DMA((8, 2)),
             DMA((2, 2)),

time: 163 us -> 141 us (0.87)
  the two profiles are of different devices: /device:TPU:2 before, /device:TPU:64 now
where the time goes in v2:
time: 141 us
  Pallas kernels  137 us (97%)
  other arithmetic  2.04 us (1%)
  local copies, waits for them, and re-layouts  1.46 us (1%)
    pallas_call x1, Pallas kernels, local(): pl.pallas_call(experts_kernel, out_shape=jax.ShapeDtypeStruct((8, D), BF)...  76.4 us
    pallas_call x1, Pallas kernels, local(): pl.pallas_call(mix_heads_kernel, out_shape=(jax.ShapeDtypeStruct((8, D),...  36.5 us
    pallas_call x1, Pallas kernels, local(): pl.pallas_call(attention_kernel, out_shape=(jax.ShapeDtypeStruct((256, D)...  24.3 us

profile of v2, /device:TPU:64, one launch (start us, length us, event | category | flops | bytes accessed | tf_op | source)
XLA Modules:
  0.0 140.7 jit_solution(13788023233730893156)
XLA Ops:
  0.0 0.1 pad.3.clone
  0.1 0.7 convert_convert_fusion
  0.8 0.7 reduce-precision_convert_fusion
  1.5 0.7 maximum_maximum_fusion.meta_ref
  2.1 24.3 %attention.1 = (bf16[256,2048]{1,0:T(8,128)(2,1)}, bf16[2048,384]{1,0:T(8,128)(2,1)}, bf16[2048,384]{1,0:T(8,128)(2,1)}, bf16[384,2048]{1,0:T(8,128)(2,1)}) custom-call(s32[4]{0:T(128)} %lengths.1, bf16[256,128]{1,0:T(8,128)(2,1)} %q_ref.1, bf16[2,256,128]{2,1,0:T(8,128)(2,1)} %k_ref.1, bf16[2,256,128]{2,1,0:T(8,128)(2,1)} %v_ref.1, ...), custom_call_target="tpu_custom_call" | custom-call | tf_op jit(solution)/shard_map/attention/pallas_call | solution.py:473
  26.4 36.5 %mix_heads.1 = (f32[8,2048]{1,0:T(8,128)}, bf16[64,1536]{1,0:T(8,128)(2,1)}) custom-call(bf16[8,4,8,2048]{3,2,1,0:T(8,128)(2,1)} %bitcast.2, bf16[8,2048]{1,0:T(8,128)(2,1)} %res_ref.1, f32[1,2048]{1,0:T(1,128)} %bitcast.3, bf16[8,128]{1,0:T(8,128)(2,1)} %maximum_maximum_fusion.meta_ref), custom_call_target="tpu_custom_call" | custom-call | tf_op jit(solution)/shard_map/mix_heads/pallas_call | solution.py:498
  62.9 76.4 %experts.1 = bf16[8,2048]{1,0:T(8,128)(2,1)} custom-call(bf16[64,1536]{1,0:T(8,128)(2,1)} %get-tuple-element.12.gy_ref, f32[8,2048]{1,0:T(8,128)} %get-tuple-element.13.stream_ref, bf16[1,2048,384]{2,1,0:T(8,128)(2,1)} %wg_ref.3, bf16[1,2048,384]{2,1,0:T(8,128)(2,1)} %wu_ref.3, bf16[1,384,2048]{2,1,0:T(8,128)(2,1)} %wd_ref.3, ...), custom_call_target="tpu_custom_call" | custom-call | tf_op jit(solution)/shard_map/experts/pallas_call | solution.py:510
  139.3 1.4 copy.14
  (1 shorter events, 0.0 us)

commit v3 on v2

--- a/solution.py
+++ b/solution.py
@@ -41,10 +41,8 @@
     pl.semaphore_wait(barrier, len(peers))
 
 
-def attention_kernel(
-    lengths, q_ref, k_ref, v_ref, wo_ref, wg_ref, wu_ref, wd_ref,
-    out_ref, pg_ref, pu_ref, pd_ref,
-    kbuf, vbuf, m_ref, l_ref, acc_ref, send, recv, wsend, wrecv,
+def attention_stage(
+    lengths, q_ref, k_ref, v_ref, att_ref, kbuf, vbuf, m_ref, l_ref, acc_ref, send, recv, pending
 ):
     a = lax.axis_index("attn")
     e = lax.axis_index("expert")
@@ -54,10 +52,8 @@
     right = ((y + 1) % RING) * 2 + c
     left = ((y + RING - 1) % RING) * 2 + c
     partner = y * 2 + (1 - c)
-    greet([{"attn": right}, {"attn": left}, {"attn": partner}])
     bufs = (kbuf, vbuf)
     ins = (k_ref, v_ref)
-    pending = []
 
     def push(kv, src, block, slot, way):
         to = (right, left, partner)[way]
@@ -73,24 +69,9 @@
             attn=partner,
         ).wait_recv()
 
-    wcopies = []
-
-    def swap(step):
-        for n, (mine, theirs, rows) in enumerate(
-            ((wg_ref, pg_ref, 512), (wu_ref, pu_ref, 512), (wd_ref, pd_ref, 96))
-        ):
-            part = pl.ds(step * rows, rows)
-            copy = remote(
-                mine.at[0, part], theirs.at[part], wsend.at[n, step], wrecv.at[n, step],
-                attn=partner,
-            )
-            copy.start()
-            wcopies.append(copy)
-
     for way in (2, 0, 1):
         for kv in range(2):
             push(kv, ins[kv].at[head], a, 0, way)
-    swap(0)
     kbuf[pl.ds(a, 1)] = k_ref[pl.ds(head, 1)]
     vbuf[pl.ds(a, 1)] = v_ref[pl.ds(head, 1)]
 
@@ -140,7 +121,6 @@
                 if step < 3 or kv == 1:
                     push(kv, bufs[kv].at[above * 2 + c], above * 2 + c, RING - step, 1)
                 push(kv, bufs[kv].at[above * 2 + c], above * 2 + c, RING - step, 2)
-            swap(step)
         else:
             for kv in range(2):
                 arrived(kv, below * 2 + c)
@@ -153,21 +133,12 @@
             def _():
                 attend(chunk)
 
-    attended = (acc_ref[...] / l_ref[...]).astype(BF)
-    for n in range(4):
-        cols = slice(n * 512, (n + 1) * 512)
-        term = jnp.dot(attended, wo_ref[:, cols], preferred_element_type=F32)
-        out_ref[:, cols] = term.astype(BF)
-    for copy in pending:
-        copy.wait_send()
-    for copy in wcopies:
-        copy.wait()
-
-
-def mix_heads_kernel(
-    ht_ref, res_ref, gain_ref, meta_ref, stream_ref, gy_ref,
-    xin, part, zin, nbuf, gbuf,
-    s1, s3, rx, rz, sy, ry,
+    att_ref[...] = (acc_ref[...] / l_ref[...]).astype(BF)
+
+
+def mix_stage(
+    att_ref, wo_ref, res_ref, gain_ref, ids_ref, gates_ref, stream_ref, toks,
+    ht_ref, xin, part, zin, nbuf, gbuf, s1, s3, rx, rz, sy, ry, pending,
 ):
     a = lax.axis_index("attn")
     e = lax.axis_index("expert")
@@ -178,11 +149,6 @@
     xs = [(x + d) % XS for d in range(XS)]
     zs = [((z + r) % RING) for r in range(RING)]
     ys = [((y + r) % RING) for r in range(RING)]
-    peers = [{"expert": z * XS + xs[d]} for d in range(1, XS)]
-    peers += [{"expert": zs[r] * XS + x} for r in range(1, RING)]
-    peers += [{"attn": ys[r] * 2 + c} for r in range(1, RING)]
-    greet(peers)
-    pending = []
 
     def push(*args, **dev):
         copy = remote(*args, **dev)
@@ -193,6 +159,11 @@
         remote(buf, buf, sem, sem, expert=z * XS + xs[1]).wait_recv()
 
     for r in ORDER:
+        part_rows = att_ref[pl.ds(pl.multiple_of(zs[r] * 32, 32), 32)]
+        for n in range(4):
+            cols = slice(n * 512, (n + 1) * 512)
+            term = jnp.dot(part_rows, wo_ref[:, cols], preferred_element_type=F32)
+            ht_ref[pl.ds(zs[r], 1), :, :, cols] = term.reshape(1, XS, 8, 512).astype(BF)
         for d in (2, 1, 3):
             push(
                 ht_ref.at[zs[r], xs[d]], xin.at[r, d - 1], s1.at[r, d - 1], rx.at[r, d - 1],
@@ -214,9 +185,15 @@
         total = total + zin[r].astype(F32)
     mean = jnp.mean(total * total, axis=1, keepdims=True)
     normalized = (total * lax.rsqrt(mean + 1e-06) * gain_ref[...]).astype(BF)
+    weight = gates_ref[...]
+    high = weight.astype(BF)
+    low = (weight - high.astype(F32)).astype(BF)
     for p in range(2):
+        nbuf[p, :, W:] = jnp.zeros((8, 128), BF)
+        nbuf[p, :, W : W + 8] = ids_ref[...].astype(F32).astype(BF)
+        nbuf[p, :, W + 8 : W + 16] = high
+        nbuf[p, :, W + 16 : W + 24] = low
         nbuf[p, :, :W] = normalized[:, p * EX : p * EX + W]
-        nbuf[p, :, W:] = meta_ref[...]
     for r in ORDER[:-1]:
         push(nbuf.at[ys[r] % 2], gbuf.at[y], sy.at[r], ry.at[r], attn=ys[r] * 2 + c)
     stream_ref[...] = total
@@ -226,18 +203,15 @@
         got(gbuf.at[src], ry.at[r])
     for n in range(4):
         pair = gbuf[2 * n : 2 * n + 2].astype(F32).reshape(16, TW)
-        gy_ref[16 * n : 16 * n + 16, :] = pair.astype(BF)
-    for copy in pending:
-        copy.wait_send()
-
-
-def experts_kernel(
-    gy_ref, stream_ref, wg_ref, wu_ref, wd_ref, pg_ref, pu_ref, pd_ref,
-    out_ref,
-    wg, wu, wd, toks, chosen, rows, mrows, act, outs, mouts, madd, fine, back, chi, clo,
+        toks[0, 16 * n : 16 * n + 16, :] = pair.astype(BF)
+
+
+def experts_stage(
+    stream_ref, out_ref, wg, wu, wd, loads,
+    toks, chosen, rows, mrows, act, outs, mouts, madd, fine, back, chi, clo,
     zsum, zgot, zlast, ysum, ygot,
-    wsem, tsend, trecv, dsend, drecv, msend, mrecv, nsend, nrecv, bsend, brecv,
-    zsend, zrecv, zfin, ysend, yrecv,
+    tsend, trecv, dsend, drecv, msend, mrecv, nsend, nrecv, bsend, brecv,
+    zsend, zrecv, zfin, ysend, yrecv, pending,
 ):
     a = lax.axis_index("attn")
     e = lax.axis_index("expert")
@@ -252,34 +226,7 @@
     down = ((z + RING - 1) % RING) * XS + x
     ys = [((y + r) % RING) for r in range(RING)]
     mate = (y + 1 - 2 * odd) * 2 + c
-    own_cols = pl.ds(pl.multiple_of(odd * EX, 128), W)
-    mate_cols = pl.ds(pl.multiple_of((1 - odd) * W, 128), EX)
     shared = pl.ds(pl.multiple_of(odd * (W - EX), 128), EX)
-    loads = []
-    for n, (mine, theirs, dst) in enumerate(
-        ((wg_ref.at[0], pg_ref, wg), (wu_ref.at[0], pu_ref, wu), (wd_ref.at[0], pd_ref, wd))
-    ):
-        for k, src in enumerate((mine, theirs)):
-            span = pl.ds(384 * k, 384)
-            if n < 2:
-                pairs = (
-                    (src.at[own_cols], dst.at[pl.ds(0, W), span]),
-                    (src.at[mate_cols], dst.at[pl.ds(W, EX), span]),
-                )
-            else:
-                pairs = (
-                    (src.at[:, own_cols], dst.at[span, pl.ds(0, W)]),
-                    (src.at[:, mate_cols], dst.at[span, pl.ds(W, EX)]),
-                )
-            for i, (from_ref, to_ref) in enumerate(pairs):
-                load = pltpu.make_async_copy(from_ref, to_ref, wsem.at[4 * n + 2 * k + i])
-                load.start()
-                loads.append(load)
-    peers = [{"expert": z * XS + xs[d]} for d in range(1, XS)]
-    peers += [{"expert": up}, {"expert": down}]
-    peers += [{"attn": ys[r] * 2 + c} for r in range(1, RING)]
-    greet(peers)
-    pending = []
 
     def push(*args, **dev):
         copy = remote(*args, **dev)
@@ -293,10 +240,9 @@
         return ref.at[slot, pl.ds(32 * h, 32)]
 
     for h in range(2):
-        own = gy_ref.at[pl.ds(32 * h, 32)]
+        own = half(toks, 0, h)
         push(own, half(toks, 1, h), tsend.at[0, h, 0], trecv.at[1, h], expert=up)
         push(own, half(toks, 7, h), tsend.at[0, h, 1], trecv.at[7, h], expert=down)
-    toks[0] = gy_ref[...]
 
     tok = lax.broadcasted_iota(jnp.int32, (64, 64), 0)
     col = lax.broadcasted_iota(jnp.int32, (64, 64), 1)
@@ -449,6 +395,61 @@
     out_ref[:, :EX] = (stream_ref[:, :EX] + evens[:, :EX]).astype(BF)
     out_ref[:, EX:W] = (stream_ref[:, EX:W] + evens[:, EX:] + odds[:, : W - EX]).astype(BF)
     out_ref[:, W:] = (stream_ref[:, W:] + odds[:, W - EX :]).astype(BF)
+
+
+def layer_kernel(
+    lengths, q_ref, k_ref, v_ref, wo_ref, wg_ref, wu_ref, wd_ref, res_ref, gain_ref,
+    ids_ref, gates_ref, out_ref,
+    kbuf, vbuf, m_ref, l_ref, acc_ref, att_ref, send, recv,
+    stream_ref, ht_ref, xin, part, zin, nbuf, gbuf, s1, s3, rx, rz, sy, ry,
+    wg, wu, wd, wsem, wsend, wrecv, toks, *rest,
+):
+    a = lax.axis_index("attn")
+    e = lax.axis_index("expert")
+    y = a // 2
+    c = a % 2
+    odd = y % 2
+    z = e // XS
+    x = e % XS
+    partner = y * 2 + (1 - c)
+    own_cols = pl.ds(pl.multiple_of(odd * EX, 128), W)
+    mate_cols = pl.ds(pl.multiple_of((1 - odd) * W, 128), EX)
+    moves = []
+    for n, (src, dst) in enumerate(((wg_ref.at[0], wg), (wu_ref.at[0], wu), (wd_ref.at[0], wd))):
+        for i, (take, put) in enumerate(((own_cols, pl.ds(0, W)), (mate_cols, pl.ds(W, EX)))):
+            for k in range(2):
+                span = pl.ds(384 * k, 384)
+                moves.append(
+                    (2 * n + i, k, src.at[take], dst.at[put, span])
+                    if n < 2
+                    else (2 * n + i, k, src.at[:, take], dst.at[span, put])
+                )
+    loads = []
+    for n, k, src, dst in moves:
+        if k == 0:
+            load = pltpu.make_async_copy(src, dst, wsem.at[n])
+            load.start()
+            loads.append(load)
+    peers = [{"attn": partner}]
+    peers += [{"attn": (y + r) % RING * 2 + c} for r in range(1, RING)]
+    peers += [{"expert": (z + r) % RING * XS + x} for r in range(1, RING)]
+    peers += [{"expert": z * XS + (x + d) % XS} for d in range(1, XS)]
+    greet(peers)
+    pending = []
+    attention_stage(
+        lengths, q_ref, k_ref, v_ref, att_ref, kbuf, vbuf, m_ref, l_ref, acc_ref, send, recv,
+        pending,
+    )
+    for n, k, src, dst in moves:
+        if k == 1:
+            swap = remote(src, dst, wsend.at[n], wrecv.at[n], attn=partner)
+            swap.start()
+            loads.append(swap)
+    mix_stage(
+        att_ref, wo_ref, res_ref, gain_ref, ids_ref, gates_ref, stream_ref, toks,
+        ht_ref, xin, part, zin, nbuf, gbuf, s1, s3, rx, rz, sy, ry, pending,
+    )
+    experts_stage(stream_ref, out_ref, wg, wu, wd, loads, toks, *rest, pending)
     for copy in pending:
         copy.wait_send()
 
@@ -464,58 +465,39 @@
     inv = pl.BlockSpec(memory_space=VM)
     anyw = pl.BlockSpec(memory_space=pl.ANY)
     smem = pl.BlockSpec(memory_space=pltpu.SMEM)
-    high = lax.reduce_precision(route_weights, 8, 7)
-    low = route_weights - high
-    meta = jnp.concatenate(
-        [expert_ids.astype(F32), high, low, jnp.zeros((8, 104), F32)], axis=1
-    ).astype(BF)
-
-    terms, pg, pu, pd = pl.pallas_call(
-        attention_kernel,
-        out_shape=(
-            jax.ShapeDtypeStruct((256, D), BF),
-            jax.ShapeDtypeStruct((D, 384), BF),
-            jax.ShapeDtypeStruct((D, 384), BF),
-            jax.ShapeDtypeStruct((384, D), BF),
-        ),
-        in_specs=[smem, inv, inv, inv, inv, anyw, anyw, anyw],
-        out_specs=(inv, anyw, anyw, anyw),
+    return pl.pallas_call(
+        layer_kernel,
+        out_shape=jax.ShapeDtypeStruct((8, D), BF),
+        in_specs=[smem, inv, inv, inv, inv, anyw, anyw, anyw, inv, inv, inv, inv],
+        out_specs=inv,
         scratch_shapes=[
             vmem(16, 256, 128),
             vmem(16, 256, 128),
             vmem(256, 1, dtype=F32),
             vmem(256, 1, dtype=F32),
             vmem(256, 128, dtype=F32),
+            vmem(256, 128),
             DMA((2, 8, 3)),
             DMA((2, 16)),
-            DMA((3, 4)),
-            DMA((3, 4)),
-        ],
-        compiler_params=pltpu.CompilerParams(collective_id=0, has_side_effects=True),
-        name="attention",
-    )(prompt_lengths, queries, keys, values, out_proj, w_gate, w_up, w_down)
-
-    stream, rows = pl.pallas_call(
-        mix_heads_kernel,
-        out_shape=(jax.ShapeDtypeStruct((8, D), F32), jax.ShapeDtypeStruct((64, TW), BF)),
-        in_specs=[inv] * 4,
-        out_specs=(inv, inv),
-        scratch_shapes=[vmem(8, 3, 8, D), vmem(8, 8, D), vmem(8, 8, D)]
-        + [vmem(2, 8, TW), vmem(8, 8, TW)]
-        + [DMA((8, 3)), DMA((8,)), DMA((8, 3)), DMA((8,)), DMA((8,)), DMA((8,))],
-        compiler_params=pltpu.CompilerParams(collective_id=1, has_side_effects=True),
-        name="mix_heads",
-    )(terms.reshape(8, 4, 8, D), residual, norm_gain.reshape(1, D), meta)
-
-    return pl.pallas_call(
-        experts_kernel,
-        out_shape=jax.ShapeDtypeStruct((8, D), BF),
-        in_specs=[inv, inv] + [anyw] * 6,
-        out_specs=inv,
-        scratch_shapes=[
+            vmem(8, D, dtype=F32),
+            vmem(8, 4, 8, D),
+            vmem(8, 3, 8, D),
+            vmem(8, 8, D),
+            vmem(8, 8, D),
+            vmem(2, 8, TW),
+            vmem(8, 8, TW),
+            DMA((8, 3)),
+            DMA((8,)),
+            DMA((8, 3)),
+            DMA((8,)),
+            DMA((8,)),
+            DMA((8,)),
             vmem(D, 768),
             vmem(D, 768),
             vmem(768, D),
+            DMA((6,)),
+            DMA((6,)),
+            DMA((6,)),
             vmem(8, 64, TW),
             vmem(8, 4, 16, W),
             vmem(8, 4, 16, W),
@@ -533,7 +515,6 @@
             vmem(2, 64, W),
             vmem(8, 8, W),
             vmem(8, 8, W),
-            DMA((12,)),
             DMA((8, 2, 2)),
             DMA((8, 2)),
             DMA((8, 3)),
@@ -550,9 +531,12 @@
             DMA((8,)),
             DMA((8,)),
         ],
-        compiler_params=pltpu.CompilerParams(collective_id=2, has_side_effects=True),
-        name="experts",
-    )(rows, stream, w_gate, w_up, w_down, pg, pu, pd)
+        compiler_params=pltpu.CompilerParams(collective_id=0, has_side_effects=True),
+        name="layer",
+    )(
+        prompt_lengths, queries, keys, values, out_proj, w_gate, w_up, w_down,
+        residual, norm_gain.reshape(1, D), expert_ids, route_weights,
+    )
 
 
 def solution(mesh):

time: 141 us -> 129 us (0.915)
  the two profiles are of different devices: /device:TPU:64 before, /device:TPU:8 now
where the time goes in v3:
time: 129 us; the launch traced here: 128 us
  Pallas kernels  127 us (98%)
  local copies, waits for them, and re-layouts  1.38 us (1%)
    pallas_call x1, Pallas kernels, local(): pl.pallas_call(layer_kernel, out_shape=jax.ShapeDtypeStruct((8, D), BF),...  127 us

profile of v3, /device:TPU:8, one launch (start us, length us, event | category | flops | bytes accessed | tf_op | source)
XLA Modules:
  0.0 128.4 jit_solution(2137893735008541772)
XLA Ops:
  0.0 127.0 %layer.1 = bf16[8,2048]{1,0:T(8,128)(2,1)} custom-call(s32[4]{0:T(128)} %lengths.1, bf16[256,128]{1,0:T(8,128)(2,1)} %q_ref.1, bf16[2,256,128]{2,1,0:T(8,128)(2,1)} %k_ref.1, bf16[2,256,128]{2,1,0:T(8,128)(2,1)} %v_ref.1, bf16[128,2048]{1,0:T(8,128)(2,1)} %wo_ref.1, bf16[1,2048,384]{2,1,0:T(8,128)(2,1)} %wg_ref.1, bf16[1,2048,384]{2,1,0:T(8,128)(2,1)} %wu_ref.1, ...), custom_call_target="tpu_custom_call" | custom-call | tf_op jit(solution)/shard_map/layer/pallas_call | solution.py:468
  127.0 1.4 %copy.14 = bf16[8,2048]{1,0:T(8,128)(2,1)} copy(bf16[8,2048]{1,0:T(8,128)(2,1)} %layer.1) | data formatting | bytes 65536

commit v4 on v3

--- a/solution.py
+++ b/solution.py
@@ -12,7 +12,7 @@
 VM = pltpu.VMEM
 DMA = pltpu.SemaphoreType.DMA
 D = 2048
-EX = 640
+EX = 768
 W = D - EX
 TW = W + 128
 CUTS = ((0, 512), (512, 1024), (1024, W))

time: 129 us -> 132 us (1.023)
  the two profiles are of different devices: /device:TPU:8 before, /device:TPU:2 now
where the time goes in v4:
time: 132 us
  Pallas kernels  130 us (98%)
  local copies, waits for them, and re-layouts  1.38 us (1%)
    pallas_call x1, Pallas kernels, local(): pl.pallas_call(layer_kernel, out_shape=jax.ShapeDtypeStruct((8, D), BF),...  130 us

profile of v4, /device:TPU:2, one launch (start us, length us, event | category | flops | bytes accessed | tf_op | source)
XLA Modules:
  0.0 131.8 jit_solution(13902747843652773626)
XLA Ops:
  0.0 130.4 %layer.1 = bf16[8,2048]{1,0:T(8,128)(2,1)} custom-call(s32[4]{0:T(128)} %lengths.1, bf16[256,128]{1,0:T(8,128)(2,1)} %q_ref.1, bf16[2,256,128]{2,1,0:T(8,128)(2,1)} %k_ref.1, bf16[2,256,128]{2,1,0:T(8,128)(2,1)} %v_ref.1, bf16[128,2048]{1,0:T(8,128)(2,1)} %wo_ref.1, bf16[1,2048,384]{2,1,0:T(8,128)(2,1)} %wg_ref.1, bf16[1,2048,384]{2,1,0:T(8,128)(2,1)} %wu_ref.1, ...), custom_call_target="tpu_custom_call" | custom-call | tf_op jit(solution)/shard_map/layer/pallas_call | solution.py:468
  130.5 1.4 %copy.14 = bf16[8,2048]{1,0:T(8,128)(2,1)} copy(bf16[8,2048]{1,0:T(8,128)(2,1)} %layer.1) | data formatting | bytes 65536
